TPU v7x, 32 devices: a whole 2x2x4 slice. The times are simulated.
32 devices in a mesh: vocab: 2 (over y), tok: 16 (over z, x, core).
Axes of the slice: x: 2, y: 2, z: 4, core: 2. Of those that a mesh axis runs over, the one named last changes fastest.
Arguments:
- hidden: bfloat16 [2048, 3584], P('tok'), may hold values from -64 to 64
- norm_gain: float32 [3584], replicated, may hold values from 0.1 to 1.9
- unembed: bfloat16 [3584, 152064], P(None, ('vocab', 'tok')), may hold values from -1 to 1
- target_ids: int32 [2048], replicated, may hold values from 0 to 152063
- loss_mask: int32 [2048], P(('vocab', 'tok')), may hold values 0 or 1
- seq_ids: int32 [2048], P(('vocab', 'tok')), may hold values from 0 to 3, never falling along the last dimension, each value on 1 to 1024 neighbouring positions
- advantages: float32 [2048], P(('vocab', 'tok')), may hold values from -20 to 20
- prox_logp: float32 [2048], P(('vocab', 'tok')), may hold values from -22 to -10
- behav_logp: float32 [2048], P(('vocab', 'tok')), may hold values from -22 to -10
Outputs:
- logp: float32 [2048], P(('vocab', 'tok'))
- token_loss: float32 [2048], P(('vocab', 'tok'))
- policy_loss: float32 [], replicated
- seq_means: float32 [2, 4], replicated
All inputs are finite; a program needn't handle non-finite values. No bound on the sum of `loss_mask` on one device may be relied on, other than what follows from the above.
Results may differ from a plain program's by a relative error of at most 0.0035.
Values may be sent and summed in bfloat16 or wider, within the bound.
A program may use at most 128 MiB of HBM per device.

v0:
```python
import jax
import jax.numpy as jnp
from jax import lax
from jax.sharding import PartitionSpec as P

LENGTH = 512


def normalize(hidden, norm_gain):
    values = hidden.astype(jnp.float32)
    scale = lax.rsqrt(jnp.mean(values * values, axis=1, keepdims=True) + 1e-06)
    return (values * scale * norm_gain).astype(jnp.bfloat16)


def block_stats(rows, unembed, targets, first_col):
    logits = jnp.dot(rows, unembed, preferred_element_type=jnp.float32)
    top = jnp.max(logits, axis=1)
    total = jnp.sum(jnp.exp(logits - top[:, None]), axis=1)
    cols = lax.broadcasted_iota(jnp.int32, logits.shape, 1)
    hit = cols == (targets - first_col)[:, None]
    picked = jnp.sum(jnp.where(hit, logits, jnp.float32(0.0)), axis=1)
    return (top, total, picked)


def place_rows(found):
    return tuple((new for new in found))


def shards(
    hidden, norm_gain, unembed, target_ids, loss_mask, seq_ids, advantages, prox_logp, behav_logp
):
    tokens = target_ids.shape[0]
    vocab_dev = unembed.shape[1]
    first_col = lax.axis_index(("vocab", "tok")) * vocab_dev
    normed = normalize(hidden, norm_gain)
    top, total, picked = place_rows(
        block_stats(
            lax.all_gather(normed, "tok", axis=0, tiled=True), unembed, target_ids, first_col
        )
    )
    share = loss_mask.shape[0]
    owned = lax.axis_index(("vocab", "tok")) * share
    peak = lax.pmax(top, ("vocab", "tok"))
    scaled = total * jnp.exp(top - peak)
    sums, picks = (
        lax.psum_scatter(scaled, ("vocab", "tok"), scatter_dimension=0, tiled=True),
        lax.psum_scatter(picked, ("vocab", "tok"), scatter_dimension=0, tiled=True),
    )
    peak_own = lax.dynamic_slice_in_dim(peak, owned, share, 0)
    logp = picks - peak_own - jnp.log(sums)
    weight_b = jnp.minimum(jnp.exp(prox_logp - behav_logp), 5.0)
    ratio = jnp.exp(logp - prox_logp)
    surr = jnp.minimum(ratio * advantages, jnp.clip(ratio, 0.8, 1.2) * advantages)
    surr = jnp.where(advantages < 0, jnp.maximum(surr, 3.0 * advantages), surr)
    token_loss = -weight_b * surr
    seqs = tokens // LENGTH
    member = (jnp.arange(seqs, dtype=jnp.int32)[:, None] == seq_ids[None, :]).astype(jnp.float32)
    member = member * loss_mask.astype(jnp.float32)[None, :]
    loss_part = jnp.sum(member * token_loss[None, :], axis=1)
    diff_part = jnp.sum(member * (logp - prox_logp)[None, :], axis=1)
    count_part = jnp.sum(member, axis=1)
    loss_sum, diff_sum, count = lax.psum((loss_part, diff_part, count_part), ("vocab", "tok"))
    policy_loss = jnp.sum(loss_sum) / jnp.maximum(jnp.sum(count), 1.0)
    floor = jnp.maximum(count, 1.0)
    seq_means = jnp.stack([loss_sum / floor, diff_sum / floor])
    return (logp, token_loss, policy_loss, seq_means)


def solution(mesh):
    in_specs = (
        P("tok", None),
        P(),
        P(None, ("vocab", "tok")),
        P(),
        P(("vocab", "tok")),
        P(("vocab", "tok")),
        P(("vocab", "tok")),
        P(("vocab", "tok")),
        P(("vocab", "tok")),
    )
    out_specs = (P(("vocab", "tok")), P(("vocab", "tok")), P(), P())
    return jax.shard_map(shards, mesh=mesh, in_specs=in_specs, out_specs=out_specs, check_vma=False)
```

profile of v0, /device:TPU:0, one launch (start us, length us, event | category | flops | bytes accessed | tf_op | source)
XLA Modules:
  0.0 355.9 jit_solution(1548288530973449643)
XLA Ops:
  7.2 0.0 all-gather.2.cloned.1.call-start
  7.2 1.4 fusion
  8.7 2.4 fusion.2
  11.1 0.0 all-gather.2.cloned.1.call-update
  11.1 1.2 convert_element_type.12
  12.3 0.7 broadcast_subtract_fusion
  13.0 114.3 %all-gather.2.cloned.1.call-done = bf16[2048,3584]{1,0:T(8,128)(2,1)} async-done(((bf16[128,3584]{1,0:T(8,128)(2,1)}), bf16[2048,3584]{1,0:T(8,128)(2,1)}) %all-gather.2.cloned.1.call-update) | async-done | bytes 14680080 | tf_op jit(solution)/shard_map/all_gather | solution.py:38
  127.3 81.2 %fusion.8 = (f32[2048]{0:T(1024)S(1)}, f32[2048,4752]{0,1:T(8,128)}) fusion(bf16[2048,3584]{1,0:T(8,128)(2,1)} %all-gather.2.cloned.1.call-done, bf16[3584,4752]{0,1:T(8,128)(2,1)} %param.11), kind=kOutput, calls=%fused_computation.25 | convolution fusion | flops 69769396224 | bytes 87678976 | tf_op jit(solution)/shard_map/dot_general | solution.py:16
  208.5 0.0 copy-start.3
  208.5 0.0 copy-start.4
  208.5 0.0 copy-start.5
  208.5 0.0 copy-start.1
  208.5 0.0 copy-start.2
  208.5 38.6 %pmax.7 = f32[2048]{0:T(1024)S(1)} all-reduce(f32[2048]{0:T(1024)S(1)} %get-tuple-element.21), channel_id=1, replica_groups=mesh['vocab'=2,'tok'=16] {'vocab','tok'}, use_global_device_ids=true, to_apply=%region_4.5 | all-reduce | flops 2048 | bytes 16384 | tf_op jit(solution)/shard_map/pmax | solution.py:43
  247.1 17.2 %select_reduce_fusion = (f32[2048]{0:T(1024)S(1)}, f32[2048]{0:T(1024)S(1)}) fusion(f32[2048,4752]{0,1:T(8,128)} %get-tuple-element.22, s32[2048]{0:T(1024)S(1)} %broadcast_subtract_fusion, f32[2048]{0:T(1024)S(1)} %get-tuple-element.21), kind=kLoop, calls=%fused_computation.1 | loop fusion | flops 48656384 | bytes 38961152 | tf_op jit(solution)/shard_map/reduce_sum | solution.py:21
  264.4 40.9 %all-reduce.3 = (f32[2048]{0:T(1024)S(1)}, f32[2048]{0:T(1024)S(1)}) all-reduce(f32[2048]{0:T(1024)S(1)} %exponential_multiply_fusion, f32[2048]{0:T(1024)S(1)} %get-tuple-element.4), channel_id=3, replica_groups=mesh['vocab'=2,'tok'=16] {'vocab','tok'}, use_global_device_ids=true, to_apply=%region_6.7.clone | all-reduce | flops 4096 | bytes 32768
  305.3 0.0 copy-done.3
  305.3 0.0 copy-done.4
  305.3 0.0 copy-done.5
  305.3 0.6 fusion.5
  305.9 0.0 copy-start
  305.9 0.0 copy-done.1
  305.9 0.0 copy-done.2
  305.9 0.1 fusion.4
  306.1 39.2 %all-reduce.2 = (f32[4]{0:T(128)S(1)}, f32[4]{0:T(128)S(1)}, f32[4]{0:T(128)S(1)}) all-reduce(f32[4]{0:T(128)S(1)} %get-tuple-element.8, f32[4]{0:T(128)S(1)} %get-tuple-element.7, f32[4]{0:T(128)S(1)} %get-tuple-element.6), channel_id=1, replica_groups=mesh['vocab'=2,'tok'=16] {'vocab','tok'}, use_global_device_ids=true, to_apply=%region_8.9 | all-reduce | flops 12 | bytes 96 | tf_op jit(solution)/shard_map/psum | solution.py:62
  345.3 0.7 divide_bitcast_fusion.1
  346.0 0.6 pad_maximum_fusion
  347.9 0.0 copy-done
  (2 shorter events, 0.0 us)
Async XLA Ops:
  7.2 120.1 %all-gather.2.cloned.1.call-start = ((), (), s32[]{:S(2)}) async-start(), calls=%async_computation | async-start | bytes 15597568 | tf_op jit(solution)/shard_map/all_gather | solution.py:38
  208.5 96.8 %copy-start.3 = (f32[64]{0:T(128)S(1)}, f32[64]{0:T(128)}, u32[]{:S(2)}) copy-start(f32[64]{0:T(128)} %param.15) | copy-start | bytes 772
  208.5 96.8 %copy-start.4 = (f32[64]{0:T(128)S(1)}, f32[64]{0:T(128)}, u32[]{:S(2)}) copy-start(f32[64]{0:T(128)} %param.16) | copy-start | bytes 772
  208.5 96.8 %copy-start.5 = (f32[64]{0:T(128)S(1)}, f32[64]{0:T(128)}, u32[]{:S(2)}) copy-start(f32[64]{0:T(128)} %param.17) | copy-start | bytes 772
  208.5 97.4 %copy-start.1 = (s32[64]{0:T(128)S(1)}, s32[64]{0:T(128)}, u32[]{:S(2)}) copy-start(s32[64]{0:T(128)} %param.14) | copy-start | bytes 772
  208.5 97.4 %copy-start.2 = (f32[64]{0:T(128)S(1)}, f32[64]{0:T(128)}, u32[]{:S(2)}) copy-start(f32[64]{0:T(128)} %convert_element_type.12) | copy-start | bytes 772
  305.9 42.0 %copy-start = (f32[64]{0:T(128)}, f32[64]{0:T(128)S(1)}, u32[]{:S(2)}) copy-start(f32[64]{0:T(128)S(1)} %get-tuple-element.14) | copy-start | bytes 772
Sparse Core Ops, SparseCore 0:
  11.2 116.0 all-gather.1
where the time goes:
time: 357 us; the launch traced here: 356 us
  blocking collectives  119 us (33%)
  waiting for transfers between devices  114 us (32%)
  matrix products  81.2 us (23%)
  other arithmetic  24.9 us (7%)
  between operations  16.6 us (5%)
    all_gather x1, waiting for transfers between devices, shards(): lax.all_gather(normed, 'tok', axis=0, tiled=True)  114 us
    dot_general x1, matrix products, block_stats(): logits = jnp.dot(rows, unembed, preferred_element_type=jnp.float32)  81.2 us
    unnamed x1, blocking collectives  40.9 us
    psum x1, blocking collectives, shards(): lax.psum((loss_part, diff_part, count_part), ('vocab', 'tok'))  39.2 us
    pmax x1, blocking collectives, shards(): peak = lax.pmax(top, ('vocab', 'tok'))  38.6 us
    reduce_sum x1, other arithmetic, block_stats(): picked = jnp.sum(jnp.where(hit, logits, jnp.float32(0.0)), axis=1)  17.2 us
  transfers between devices with their start and end apart: 1, of which 1 were waited for; matrix products, arithmetic and copies ran while one was open for 1% of the time, Pallas kernels for 0%

commit v1 on v0

v1 whole, which is shorter than its diff:
```python
import jax
import jax.numpy as jnp
from jax import lax
from jax.experimental import pallas as pl
from jax.experimental.pallas import tpu as pltpu
from jax.sharding import PartitionSpec as P

LENGTH = 512
LANES = 128
HALVES = 2
LOW = -1e30
MESH = pl.DeviceIdType.MESH


def sections_of(columns):
    tiles = (columns + 255) // 256
    parts = 3 if tiles >= 3 else 1
    cuts = [tiles * i // parts * 256 for i in range(parts)] + [columns]
    return [(cuts[i], cuts[i + 1] - cuts[i]) for i in range(parts)]


def padded(width):
    return (width + LANES - 1) // LANES * LANES


def pick(index, values):
    found = values[0]
    for k in range(1, len(values)):
        found = jnp.where(index == k, values[k], found)
    return found


def make_kernel(n_vocab, n_tok, rows, depth, columns, tokens, share, seqs):
    na = n_tok // 4
    n_dev = n_vocab * n_tok
    secs = sections_of(columns)
    n_sec = len(secs)
    half = rows // HALVES
    per_tile = LANES // share
    pairs = rows * 2
    steps_of = [(1, 0), (0, 1)] if na > 2 else [(0, 1)]
    for i in range(2, na - 1):
        steps_of += [(i, 0), (i - 1, 1)]
    if na > 2:
        steps_of += [(na - 2, 1)]
    n_step = 3 + len(steps_of)
    step_at = {item: 3 + k for k, item in enumerate(steps_of)}
    step_at[(0, 0)] = 2

    def z_time(d, h):
        return [(2, 3), (5, 6), (9, 10)][d - 1][h] if d <= 3 else 3 * (2 * d - 3) + h

    def kernel(hidden, gain, weights, ids, mask, seq, adv, prox, behav,
               logp_out, loss_out, policy_out, means_out,
               x, w, logits, m_ref, s_ref, p_ref, t_ref, stats, got, tile, tiles,
               w_sem, recv, send, st_send, st_recv, ls_send, ls_recv):
        v = lax.axis_index("vocab")
        t = lax.axis_index("tok")
        me = v * n_tok + t
        c = t % 2
        b = (t // 2) % 2
        a = t // 4
        plane = v % 2
        active = c == plane
        passive = c != plane

        loads = [pltpu.make_async_copy(weights.at[:, pl.ds(lo, n)], w[k], w_sem.at[k])
                 for k, (lo, n) in enumerate(secs)]
        for load in loads:
            load.start()
        barrier = pltpu.get_barrier_semaphore()

        @pl.loop(0, n_dev)
        def _(other):
            @pl.when(other != me)
            def _():
                pl.semaphore_signal(barrier, inc=1, device_id=(other // n_tok, other % n_tok), device_id_type=MESH)

        @pl.loop(0, rows // 16)
        def _(r):
            at = pl.ds(pl.multiple_of(r * 16, 16), 16)
            values = hidden[at, :].astype(jnp.float32)
            scale = lax.rsqrt(jnp.mean(values * values, axis=1, keepdims=True) + 1e-06)
            x[t, at, :] = (values * scale * gain[...]).astype(jnp.bfloat16)

        for k in range(n_sec):
            logits[k][...] = jnp.zeros_like(logits[k])
        m_ref[...] = jnp.full_like(m_ref, LOW)
        s_ref[...] = jnp.zeros_like(s_ref)
        p_ref[...] = jnp.zeros_like(p_ref)
        t_ref[...] = jnp.full_like(t_ref, -1)
        stats[...] = jnp.zeros_like(stats)
        pl.semaphore_wait(barrier, n_dev - 1)

        def slot_of(sa, sb, sc):
            return sa * 4 + sb * 2 + sc

        def other_row(i):
            up = i + jnp.where(i >= a, 1, 0)
            mirror = na - 1 - a
            down = na - 1 - (i + jnp.where(i >= mirror, 1, 0))
            return jnp.where(a * 2 < na, up, down)

        def piece(slot, h, way, dv, dt):
            ref = x.at[slot, pl.ds(h * half, half), :]
            return pltpu.make_async_remote_copy(
                src_ref=ref, dst_ref=ref, send_sem=send.at[way, slot, h], recv_sem=recv.at[slot, h],
                device_id=(dv, dt), device_id_type=MESH)

        closing = []

        def ship(when, pred, slot, h, way, dv, dt):
            @pl.when(pred if when is None else jnp.logical_and(when, pred))
            def _():
                copy = piece(slot, h, way, dv, dt)
                if closing:
                    copy.wait_send()
                else:
                    copy.start()

        def take(when, pred, slot, h):
            if not closing:
                @pl.when(jnp.logical_and(when, pred))
                def _():
                    piece(slot, h, 0, v, t + 1 - 2 * c).wait_recv()

        flip_v = v + 1 - 2 * plane
        mate = t + 1 - 2 * c
        beside = slot_of(a, 1 - b, c)
        events = {}

        def on(q, fn):
            events.setdefault(q, []).append(fn)

        def to_mate(when, pred, slot, h):
            ship(when, pred, slot, h, 4, v, mate)

        def own_x(pred):
            def fn(when):
                for h in range(HALVES):
                    ship(when, pred, t, h, 2, v, beside)
            return fn

        on(3, own_x(passive))

        def z_take(d, h):
            def fn(when):
                for side in (-1, 1):
                    far = a + side * d
                    there = jnp.logical_and(far >= 0, far < na)
                    pred = jnp.logical_and(active, there)
                    slot = slot_of(jnp.clip(far, 0, na - 1), b, c)

                    take(when, pred, slot, h)
                    nxt = a - side
                    go = jnp.logical_and(pred, jnp.logical_and(nxt >= 0, nxt < na))
                    ship(when, go, slot, h, 0 if side > 0 else 1, v, slot_of(jnp.clip(nxt, 0, na - 1), b, c))
                    to_mate(when, pred, slot, h)
            return fn

        def beside_take(pred, h):
            def fn(when):
                take(when, pred, beside, h)
                to_mate(when, pred, beside, h)
            return fn

        def x_send(i, h):
            return lambda when: ship(when, active, slot_of(other_row(i), b, c), h, 2, v, beside)

        def y_send(i, e, h):
            return lambda when: ship(when, active, slot_of(other_row(i), b if e == 0 else 1 - b, c), h, 3, flip_v, t)

        def x_take(i, h):
            def fn(when):
                slot = slot_of(other_row(i), 1 - b, c)
                take(when, active, slot, h)
                to_mate(when, active, slot, h)
            return fn

        def y_take(i, e, h):
            def fn(when):
                slot = slot_of(other_row(i), b if e == 0 else 1 - b, c)
                take(when, passive, slot, h)
                to_mate(when, passive, slot, h)
            return fn

        for h in range(HALVES):
            on(2 + h, beside_take(active, h))
            on(5 + h, beside_take(passive, h))
        for d in range(1, na):
            for h in range(HALVES):
                on(z_time(d, h), z_take(d, h))
        for i in range(na - 1):
            for h in range(HALVES):
                zt = z_time(i + 1, h)
                on(max(zt, 5), x_send(i, h))
                on(zt, y_send(i, 0, h))
                xt = 3 * step_at[(i, 1)] - (4 if i == 0 else 7) + h
                on(xt, x_take(i, h))
                on(xt, y_send(i, 1, h))
                for e in (0, 1):
                    yt = 3 * step_at[(i, e)] - (1 - h)
                    if (i, e) == (0, 0):
                        yt = (4, 6)[h]
                    on(yt, y_take(i, e, h))

        def open_sends():
            for h in range(HALVES):
                to_mate(None, me >= 0, t, h)
                for side in (-1, 1):
                    nxt = a - side
                    go = jnp.logical_and(active, jnp.logical_and(nxt >= 0, nxt < na))
                    ship(None, go, t, h, 0 if side > 0 else 1, v, slot_of(jnp.clip(nxt, 0, na - 1), b, c))
            own_x(active)(None)

        open_sends()

        def slots_at(s):
            first = [slot_of(a, b, 0), slot_of(a, 1 - b, plane), slot_of(a, 1 - b, 1 - plane)]
            second = [slot_of(a, b, 1), slot_of(other_row(0), b, plane), slot_of(other_row(0), b, 1 - plane)]
            for i, e in steps_of:
                sb = b if e == 0 else 1 - b
                first.append(slot_of(other_row(i), sb, 0))
                second.append(slot_of(other_row(i), sb, 1))
            return pick(s, first), pick(s, second)

        first_col = me * columns
        lane = lax.broadcasted_iota(jnp.int32, (LANES, LANES), 1)
        group = 64

        def absorb(k):
            lo, n = secs[k]
            count = padded(n) // LANES
            ref = logits[k]
            lanes = lax.broadcasted_iota(jnp.int32, (group, LANES), 1)
            for r in range(0, pairs, group):
                at = slice(r, r + group)

                def value(j):
                    found = ref[at, j * LANES:(j + 1) * LANES]
                    left = n - j * LANES
                    return found if left >= LANES else jnp.where(lanes < left, found, LOW)
                old = m_ref[at, :]
                new = old
                chosen = p_ref[at, :]
                where = t_ref[at, :]
                for j in range(count):
                    item = value(j)
                    new = jnp.maximum(new, item)
                    hit = where == lo + j * LANES
                    if n - j * LANES < LANES:
                        hit = jnp.logical_and(hit, lanes < n - j * LANES)
                    chosen = jnp.where(hit, item, chosen)
                total = s_ref[at, :] * jnp.exp(old - new)
                for j in range(count):
                    total = total + jnp.exp(value(j) - new)
                m_ref[at, :] = new
                s_ref[at, :] = total
                p_ref[at, :] = chosen

        def stat_copy(slot, o):
            return pltpu.make_async_remote_copy(
                src_ref=stats.at[slot], dst_ref=got.at[me], send_sem=st_send.at[o], recv_sem=st_recv.at[me],
                device_id=(o // n_tok, o % n_tok), device_id_type=MESH)

        def settle(s):
            for k, slot in enumerate(slots_at(s)):
                at = slice(k * rows, (k + 1) * rows)
                m = m_ref[at, :].T
                top = jnp.max(m, axis=0, keepdims=True)
                total = jnp.sum(s_ref[at, :].T * jnp.exp(m - top), axis=0, keepdims=True)
                chosen = jnp.sum(p_ref[at, :].T, axis=0, keepdims=True)
                stats[slot, 0:1, :] = top
                stats[slot, 1:2, :] = total
                stats[slot, 2:3, :] = chosen
            for k, slot in enumerate(slots_at(s)):
                for g in range(per_tile):
                    o = slot * per_tile + g

                    @pl.when(o != me)
                    def _():
                        stat_copy(slot, o).start()

        def begin(s):
            for k, slot in enumerate(slots_at(s)):
                at = slice(k * rows, (k + 1) * rows)
                line = jnp.broadcast_to(ids[pl.ds(slot, 1), :], (LANES, LANES))
                t_ref[at, :] = line.T - first_col - lane
            m_ref[...] = jnp.full_like(m_ref, LOW)
            s_ref[...] = jnp.zeros_like(s_ref)
            p_ref[...] = jnp.zeros_like(p_ref)

        def run_step(s, carry):
            one, two = slots_at(s)
            for point in range(3):
                for q in sorted(events):
                    if q % 3 == point:
                        when = s == q // 3
                        for fn in events[q]:
                            fn(when)
                if point == 0:
                    for slot in (one, two):
                        for h in range(HALVES):
                            take(s >= 0, slot % 2 != c, slot, h)
                if point < n_sec:
                    @pl.when(s == 0)
                    def _():
                        loads[point].wait()
                    lo, n = secs[point]
                    block = jnp.concatenate([x[one], x[two]], axis=0)
                    logits[point][:, 0:n] = jnp.dot(block, w[point][...], preferred_element_type=jnp.float32)
                    absorb((point - 1) % n_sec)
                    if point == 0:
                        @pl.when(s > 0)
                        def _():
                            settle(s - 1)
                        begin(s)
            return carry

        lax.fori_loop(0, n_step, run_step, 0)
        absorb(n_sec - 1)
        settle(n_step - 1)

        mine = me // per_tile
        got[me, :, :] = stats[mine]

        @pl.loop(0, n_dev)
        def _(o):
            @pl.when(o != me)
            def _():
                pltpu.make_async_remote_copy(
                    src_ref=stats.at[mine], dst_ref=got.at[o], send_sem=st_send.at[o], recv_sem=st_recv.at[o],
                    device_id=(o // n_tok, o % n_tok), device_id_type=MESH).wait_recv()

        peak = jnp.full((8, LANES), LOW, jnp.float32)
        for o in range(n_dev):
            peak = jnp.maximum(peak, got[o])
        peak = peak[0:1, :]
        total = jnp.zeros((1, LANES), jnp.float32)
        chosen = jnp.zeros((1, LANES), jnp.float32)
        for o in range(n_dev):
            total = total + got[o, 1:2, :] * jnp.exp(got[o, 0:1, :] - peak)
            chosen = chosen + got[o, 2:3, :]
        wide = chosen - peak - jnp.log(total)
        logp = wide[:, 0:share]
        for g in range(1, per_tile):
            logp = jnp.where(me % per_tile == g, wide[:, g * share:(g + 1) * share], logp)
        prox_v = prox[...]
        adv_v = adv[...]
        weight_b = jnp.minimum(jnp.exp(prox_v - behav[...]), 5.0)
        ratio = jnp.exp(logp - prox_v)
        surr = jnp.minimum(ratio * adv_v, jnp.clip(ratio, 0.8, 1.2) * adv_v)
        surr = jnp.where(adv_v < 0, jnp.maximum(surr, 3.0 * adv_v), surr)
        token_loss = -weight_b * surr
        logp_out[...] = logp
        loss_out[...] = token_loss
        live = mask[...].astype(jnp.float32)
        tile[...] = jnp.zeros_like(tile)
        for i in range(seqs):
            member = jnp.where(seq[...] == i, live, 0.0)
            for k, part in enumerate((member * token_loss, member * (logp - prox_v), member)):
                tile[k * seqs + i:k * seqs + i + 1, 0:share] = part
        tiles[me, :, :] = tile[...]

        def loss_copy(o, where):
            return pltpu.make_async_remote_copy(
                src_ref=tile, dst_ref=tiles.at[where], send_sem=ls_send.at[o], recv_sem=ls_recv.at[where],
                device_id=(o // n_tok, o % n_tok), device_id_type=MESH)

        @pl.loop(0, n_dev)
        def _(o):
            @pl.when(o != me)
            def _():
                loss_copy(o, me).start()

        closing.append(True)
        open_sends()
        for q in sorted(events):
            for fn in events[q]:
                fn(None)

        @pl.loop(0, n_dev)
        def _(o):
            @pl.when(o != me)
            def _():
                stat_copy(o // per_tile, o).wait_send()
                loss_copy(o, o).wait()

        summed = tiles[0]
        for o in range(1, n_dev):
            summed = summed + tiles[o]
        sums = jnp.sum(summed, axis=1, keepdims=True)
        loss_sum, diff_sum, count = (sums[k * seqs:(k + 1) * seqs] for k in range(3))
        policy_out[...] = jnp.sum(loss_sum, axis=0, keepdims=True) / jnp.maximum(jnp.sum(count, axis=0, keepdims=True), 1.0)
        floor = jnp.maximum(count, 1.0)
        means_out[:, 0:1] = loss_sum / floor
        means_out[:, 1:2] = diff_sum / floor

    tile_rows = (3 * seqs + 7) // 8 * 8
    scratch = [
        pltpu.VMEM((n_tok, rows, depth), jnp.bfloat16),
        [pltpu.VMEM((depth, n), jnp.bfloat16) for _, n in secs],
        [pltpu.VMEM((pairs, padded(n)), jnp.float32) for _, n in secs],
        pltpu.VMEM((pairs, LANES), jnp.float32),
        pltpu.VMEM((pairs, LANES), jnp.float32),
        pltpu.VMEM((pairs, LANES), jnp.float32),
        pltpu.VMEM((pairs, LANES), jnp.int32),
        pltpu.VMEM((n_tok, 8, LANES), jnp.float32),
        pltpu.VMEM((n_dev, 8, LANES), jnp.float32),
        pltpu.VMEM((tile_rows, LANES), jnp.float32),
        pltpu.VMEM((n_dev, tile_rows, LANES), jnp.float32),
        pltpu.SemaphoreType.DMA((n_sec,)),
        pltpu.SemaphoreType.DMA((n_tok, HALVES)),
        pltpu.SemaphoreType.DMA((5, n_tok, HALVES)),
        pltpu.SemaphoreType.DMA((n_dev,)),
        pltpu.SemaphoreType.DMA((n_dev,)),
        pltpu.SemaphoreType.DMA((n_dev,)),
        pltpu.SemaphoreType.DMA((n_dev,)),
    ]
    return kernel, scratch


def solution(mesh):
    n_vocab, n_tok = mesh.shape["vocab"], mesh.shape["tok"]

    def shards(hidden, norm_gain, unembed, target_ids, loss_mask, seq_ids, advantages, prox_logp, behav_logp):
        rows, depth = hidden.shape
        columns = unembed.shape[1]
        tokens = target_ids.shape[0]
        share = loss_mask.shape[0]
        seqs = tokens // LENGTH
        kernel, scratch = make_kernel(n_vocab, n_tok, rows, depth, columns, tokens, share, seqs)
        vmem = pl.BlockSpec(memory_space=pltpu.VMEM)
        logp, token_loss, policy, means = pl.pallas_call(
            kernel,
            out_shape=(
                jax.ShapeDtypeStruct((1, share), jnp.float32),
                jax.ShapeDtypeStruct((1, share), jnp.float32),
                jax.ShapeDtypeStruct((1, 1), jnp.float32),
                jax.ShapeDtypeStruct((seqs, 2), jnp.float32),
            ),
            in_specs=[vmem, vmem, pl.BlockSpec(memory_space=pl.ANY)] + [vmem] * 6,
            out_specs=(vmem,) * 4,
            scratch_shapes=scratch,
            compiler_params=pltpu.CompilerParams(collective_id=0, has_side_effects=True, vmem_limit_bytes=67043328),
        )(
            hidden, norm_gain.reshape(1, depth), unembed, target_ids.reshape(n_tok, rows),
            *(item.reshape(1, share) for item in (loss_mask, seq_ids, advantages, prox_logp, behav_logp)),
        )
        return logp.reshape(share), token_loss.reshape(share), policy.reshape(()), means.T

    both = P(("vocab", "tok"))
    in_specs = (P("tok", None), P(), P(None, ("vocab", "tok")), P(), both, both, both, both, both)
    return jax.shard_map(shards, mesh=mesh, in_specs=in_specs, out_specs=(both, both, P(), P()), check_vma=False)
```

time: 357 us -> 173 us (0.48)
  Pallas kernels: 0 us -> 120 us
  blocking collectives: 119 us -> 0 us
  waiting for transfers between devices: 114 us -> 0 us
  matrix products: 81.2 us -> 0 us
  local copies, waits for them, and re-layouts: 0.03 us -> 47.8 us
  other arithmetic: 24.9 us -> 0 us
  between operations: 16.6 us -> 2.34 us
    pallas_call x0 -> x1, Pallas kernels: none -> 120 us  [shards(): pl.pallas_call(kernel, out_shape=(jax.ShapeDtypeStruct((1, share), jnp.fl...]
    all_gather x1 -> x0, waiting for transfers between devices: 114 us -> none  [shards(): lax.all_gather(normed, 'tok', axis=0, tiled=True)]
    dot_general x1 -> x0, matrix products: 81.2 us -> none  [block_stats(): logits = jnp.dot(rows, unembed, preferred_element_type=jnp.float32)]
    unnamed x12 -> x4, local copies, waits for them, and re-layouts: 0.03 us -> 46.5 us
    unnamed x1 -> x0, blocking collectives: 40.9 us -> none
    psum x1 -> x0, blocking collectives: 39.2 us -> none  [shards(): lax.psum((loss_part, diff_part, count_part), ('vocab', 'tok'))]
    pmax x1 -> x0, blocking collectives: 38.6 us -> none  [shards(): peak = lax.pmax(top, ('vocab', 'tok'))]
    reduce_sum x3 -> x0, other arithmetic: 18.8 us -> none  [the longest x1 17.2 us: block_stats(): picked = jnp.sum(jnp.where(hit, logits, jnp.float32(0.0)), axis=1)]
  transfers between devices with their start and end apart: 1 -> 0, of which waited for: 1 -> 0; matrix products, arithmetic and copies ran while one was open for 1% -> 0% of each run, Pallas kernels for 0% -> 0%
where the time goes in v1:
time: 173 us; the launch traced here: 171 us
  Pallas kernels  120 us (69%)
  local copies, waits for them, and re-layouts  47.8 us (28%)
  between operations  2.34 us (1%)
    pallas_call x1, Pallas kernels, shards(): pl.pallas_call(kernel, out_shape=(jax.ShapeDtypeStruct((1, share), jnp.fl...  120 us
    unnamed x4, local copies, waits for them, and re-layouts  46.5 us

profile of v1, /device:TPU:0, one launch (start us, length us, event | category | flops | bytes accessed | tf_op | source)
XLA Modules:
  0.0 170.6 jit_solution(8350988792220553573)
XLA Ops:
  0.6 1.3 reshape.38.gain
  2.0 42.9 %copy.13.weights = bf16[3584,4752]{1,0:T(8,128)(2,1)} copy(bf16[3584,4752]{0,1:T(8,128)(2,1)} %param.11) | data formatting | bytes 68124672 | tf_op args[2]
  44.8 120.5 %shard_map.120 = (f32[1,64]{1,0:T(1,128)}, f32[1,64]{1,0:T(1,128)}, f32[1,1]{1,0:T(1,128)}, f32[4,2]{1,0:T(4,128)}) custom-call(bf16[128,3584]{1,0:T(8,128)(2,1)} %hidden.1, f32[1,3584]{1,0:T(1,128)} %reshape.38.gain, bf16[3584,4752]{1,0:T(8,128)(2,1)} %copy.13.weights, s32[16,128]{1,0:T(8,128)} %bitcast.10, s32[1,64]{1,0:T(1,128)} %bitcast.12, ...), custom_call_target="tpu_custom_call" | custom-call | tf_op jit(solution)/shard_map/pallas_call | solution.py:434
  165.3 1.3 copy.14
  166.6 1.2 copy.18
  167.8 1.1 copy.19
